TPU v7x, 32 devices: a whole 2x2x4 slice. The times are simulated.
32 devices in a mesh: ctx: 2 (over x), grp: 4 (over y, core), tp: 4 (over z).
Axes of the slice: x: 2, y: 2, z: 4, core: 2. Of those that a mesh axis runs over, the one named last changes fastest.
Arguments:
- tokens: bfloat16 [4096, 4608], P(('grp', 'ctx')), parts along dimension 0, may hold values from -6 to 6
- token_pos: int32 [4096], P(('grp', 'ctx')), parts along dimension 0, may hold values from 0 to 1023, as said below
- norm_gain: float32 [4608], replicated, may hold values from 0.1 to 1.9
- query_weight: bfloat16 [4608, 4096], P('ctx', 'tp'), may hold values from -0.09375 to 0.09375
- key_weight: bfloat16 [4608, 2048], P('ctx', 'tp'), may hold values from -0.09375 to 0.09375
- value_weight: bfloat16 [4608, 2048], P('ctx', 'tp'), may hold values from -0.09375 to 0.09375
Outputs:
- attended: bfloat16 [4096, 4096], P(('grp', 'ctx'), 'tp'), parts along dimension 0
There are 4 independent parts, one for each index of `grp`. A program takes and returns all parts, laid end to end along the dimension named above; an argument that names none is the same for every part. Nothing has to cross between parts.
Inputs may be any that keep to these rules, and one draw needn't show every extreme that they name: `token_pos`: the 512 rows of each index of ctx form two runs of 256 consecutive ascending positions, each starting at a multiple of 256; every position of the sequence occurs exactly once.
All inputs are finite; a program needn't handle non-finite values.
Results may differ from a plain program's by a relative error of at most 0.0077.
Values may be sent and summed in bfloat16 or wider, within the bound.
A program may use at most 128 MiB of HBM per device.

v0:
```python
import functools
import math

import jax
import jax.numpy as jnp
import numpy as np
from jax import lax
from jax.experimental import pallas as pl
from jax.experimental.pallas import tpu as pltpu
from jax.sharding import PartitionSpec as P

HEAD_DIM = 128
BLOCK = 2 * HEAD_DIM
MESH = pl.DeviceIdType.MESH

query_scale = 144.0 ** (-0.5)


def each(start, stop, body):
    if stop - start == 1:
        body(start)
    elif stop > start:
        lax.fori_loop(start, stop, lambda i, _: (body(i), None)[1], None)


def kernel(
    n, grp, pos_ref, freq_ref, gain_ref, tok_ref, q_ref, k_ref, v_ref, out_ref,
    wbuf, normed, kvbuf, posbuf, qbuf, acc, cos_ref, sin_ref, qpos_ref,
    tok_sem, own_sem, x_send, x_recv, y_send, y_recv, s_send, s_recv, t_send, t_recv,
    kv_send, kv_recv, pos_send, pos_recv,
):
    c = lax.axis_index("ctx")
    g = lax.axis_index("grp")
    pairs = grp // 2
    near = g % 2
    pair = g // 2
    sibling = pair * 2 + (1 - near)
    depth = q_ref.shape[0]
    part = depth // grp
    rows = tok_ref.shape[0]
    kv_blocks = k_ref.shape[1] // BLOCK
    groups = k_ref.shape[1] // HEAD_DIM
    q_blocks = q_ref.shape[1] // BLOCK
    sources = [(k_ref, i) for i in range(kv_blocks)]
    sources += [(v_ref, i) for i in range(kv_blocks)]
    sources += [(q_ref, i) for i in range(q_blocks)]
    blocks = len(sources)

    def region(owner, member):
        return pl.ds(pl.multiple_of(owner * depth + member * part, 16), part)

    def peer(d):
        return lax.rem(c + d, n)

    def source(d):
        return lax.rem(c + n - d, n)

    def far(j):
        return lax.rem(pair + j, pairs)

    def near_of(j):
        return lax.rem(pair + pairs - j, pairs)

    def x_copy(b, d):
        return pltpu.make_async_remote_copy(
            src_ref=wbuf.at[b, region(c, g)], dst_ref=wbuf.at[b, region(c, g)],
            send_sem=x_send.at[b, d - 1], recv_sem=x_recv.at[b, d - 1],
            device_id={"ctx": peer(d)}, device_id_type=MESH,
        )

    def hop(b, where, send, recv, member):
        return pltpu.make_async_remote_copy(
            src_ref=wbuf.at[b, where], dst_ref=wbuf.at[b, where],
            send_sem=send, recv_sem=recv, device_id={"grp": member}, device_id_type=MESH,
        )

    def y_copy(b, d, j):
        return hop(b, region(source(d), g), y_send.at[b, d - 1, j - 1], y_recv.at[b, d - 1, j - 1],
                   far(j) * 2 + near)

    def y_wait(b, d, j):
        hop(b, region(source(d), near_of(j) * 2 + near), y_send.at[b, d - 1, j - 1],
            y_recv.at[b, d - 1, j - 1], sibling).wait_recv()

    def s_copy(b, d):
        return hop(b, region(source(d), g), s_send.at[b, d - 1], s_recv.at[b, d - 1], sibling)

    def s_wait(b, d):
        hop(b, region(source(d), sibling), s_send.at[b, d - 1], s_recv.at[b, d - 1],
            sibling).wait_recv()

    def t_copy(b, d, j):
        return hop(b, region(source(d), near_of(j) * 2 + near), t_send.at[b, d - 1, j - 1],
                   t_recv.at[b, d - 1, j - 1], sibling)

    def t_wait(b, d, j):
        hop(b, region(source(d), near_of(j) * 2 + 1 - near), t_send.at[b, d - 1, j - 1],
            t_recv.at[b, d - 1, j - 1], sibling).wait_recv()

    def kv_copy(b, d, owner):
        return pltpu.make_async_remote_copy(
            src_ref=kvbuf.at[b, owner], dst_ref=kvbuf.at[b, owner],
            send_sem=kv_send.at[b, d - 1], recv_sem=kv_recv.at[b, d - 1],
            device_id={"ctx": peer(d)}, device_id_type=MESH,
        )

    def pos_copy(d, owner):
        return pltpu.make_async_remote_copy(
            src_ref=posbuf.at[owner], dst_ref=posbuf.at[owner],
            send_sem=pos_send.at[d - 1], recv_sem=pos_recv.at[d - 1],
            device_id={"ctx": peer(d)}, device_id_type=MESH,
        )

    def own_copy(b):
        ref, col = sources[b]
        return pltpu.make_async_copy(
            ref.at[:, pl.ds(col * BLOCK, BLOCK)],
            wbuf.at[b, pl.ds(pl.multiple_of(c * depth, 16), depth)], own_sem.at[b],
        )

    tok_copy = pltpu.make_async_copy(tok_ref, normed, tok_sem)
    own_copy(0).start()
    own_copy(1).start()
    tok_copy.start()
    for b in range(2, blocks):
        own_copy(b).start()

    barrier = pltpu.get_barrier_semaphore()

    def greet(**where):
        pl.semaphore_signal(barrier, inc=1, device_id=where, device_id_type=MESH)

    each(1, n, lambda d: greet(ctx=peer(d)))
    each(1, pairs, lambda j: greet(grp=far(j) * 2 + near))
    greet(grp=sibling)
    pl.semaphore_wait(barrier, n - 1 + pairs - 1 + 1)

    def send_block(b):
        own_copy(b).wait()
        each(1, n, lambda d: x_copy(b, d).start())

    send_block(0)
    send_block(1)

    lanes = pos_ref[...][None, :]
    posbuf[c] = jnp.broadcast_to(lanes, posbuf.shape[1:])
    qpos = jnp.transpose(
        jnp.broadcast_to(lanes.astype(jnp.float32), (HEAD_DIM, rows)), (1, 0)
    )
    qpos_ref[...] = qpos
    angle = qpos * freq_ref[...]
    lane = lax.broadcasted_iota(jnp.int32, angle.shape, 1)
    sine = jnp.sin(angle)
    cos_ref[...] = jnp.cos(angle)
    sin_ref[...] = jnp.where(lane < HEAD_DIM // 2, -sine, sine)

    tok_copy.wait()
    strip = 32

    def norm_rows(i):
        where = pl.ds(pl.multiple_of(i * strip, strip), strip)
        inputs = normed[where, :].astype(jnp.float32)
        mean = jnp.mean(inputs * inputs, -1, keepdims=True)
        normed[where, :] = (inputs * lax.rsqrt(mean + 1e-06) * gain_ref[...][None, :]).astype(jnp.bfloat16)

    each(0, rows // strip, norm_rows)

    tall = math.gcd(rows, 256)

    def project(b, store, rope, scale):
        def tile(i):
            where = pl.ds(pl.multiple_of(i * tall, tall), tall)
            field = jnp.dot(normed[where, :], wbuf[b], preferred_element_type=jnp.float32)
            if rope:
                cosine, sine = cos_ref[where, :], sin_ref[where, :]
                halves = []
                for h in range(2):
                    one = field[:, h * HEAD_DIM : (h + 1) * HEAD_DIM]
                    halves.append(one * cosine + pltpu.roll(one, HEAD_DIM // 2, 1) * sine)
                field = jnp.concatenate(halves, -1)
            if scale is not None:
                field = field * scale
            store(where, field.astype(jnp.bfloat16))

        each(0, rows // tall, tile)

    def attend(b, owner, first, last):
        def tile(i):
            where = pl.ds(pl.multiple_of(i * tall, tall), tall)
            keys = kvbuf[b, owner]
            values = kvbuf[groups + b, owner]
            values = jnp.concatenate([values, jnp.ones_like(values)], -1)
            key_pos = posbuf[owner, 0:1, :].astype(jnp.float32)
            allowed = key_pos <= qpos_ref[where, 0:1]
            for h in range(2):
                cols = pl.ds(h * HEAD_DIM, HEAD_DIM)
                scores = lax.dot_general(
                    qbuf[b, where, cols], keys, (((1,), (1,)), ((), ())),
                    preferred_element_type=jnp.float32,
                )
                capped = jnp.tanh(scores * (1.0 / 50.0)) * (50.0 * math.log2(math.e))
                weights = jnp.where(allowed, jnp.exp2(capped), 0.0).astype(jnp.bfloat16)
                both = jnp.dot(weights, values, preferred_element_type=jnp.float32)
                if not first:
                    both = both + acc[b, h, where, :]
                if last:
                    done = both[:, :HEAD_DIM] / both[:, HEAD_DIM:]
                    out_ref[where, pl.ds(b * BLOCK + h * HEAD_DIM, HEAD_DIM)] = done.astype(
                        out_ref.dtype
                    )
                else:
                    acc[b, h, where, :] = both

        each(0, rows // tall, tile)

    received = set()

    def attend_others(b):
        if "pos" not in received:
            received.add("pos")
            each(1, n, lambda d: pos_copy(d, source(d)).wait_recv())
        for index in (b, groups + b):
            if index not in received:
                received.add(index)
                each(1, n, lambda d: kv_copy(index, d, source(d)).wait_recv())
        each(1, n - 1, lambda d: attend(b, source(d), False, False))
        attend(b, source(n - 1), False, True)

    def send_group(h):
        each(1, n, lambda d: kv_copy(h, d, c).start())
        each(1, n, lambda d: kv_copy(groups + h, d, c).start())

    def store_kv(first):
        def store(where, field):
            kvbuf[first, c, where, :] = field[:, :HEAD_DIM]
            kvbuf[first + 1, c, where, :] = field[:, HEAD_DIM:]

        return store

    def store_q(h):
        def store(where, field):
            qbuf[h, where, :] = field

        return store

    for t in range(blocks + 2):
        if t < blocks:
            def forward(d, b=t):
                x_copy(b, d).wait_recv()
                each(1, pairs, lambda j: y_copy(b, d, j).start())
                s_copy(b, d).start()

            each(1, n, forward)
        if 1 <= t <= blocks:
            def onward(d, b=t - 1):
                def one(j):
                    y_wait(b, d, j)
                    t_copy(b, d, j).start()

                each(1, pairs, one)

            each(1, n, onward)
        if t >= 2:
            b = t - 2

            def arrive(d, b=b):
                s_wait(b, d)
                each(1, pairs, lambda j: t_wait(b, d, j))

            each(1, n, arrive)
            if b < 2 * kv_blocks:
                project(b, store_kv(2 * b), b < kv_blocks, None)
        if t + 2 < blocks:
            send_block(t + 2)
        if t == 2:
            each(1, n, lambda d: pos_copy(d, c).start())
        if t >= blocks - 2:
            share = [h for h in range(groups) if min(blocks - 2 + h, blocks) == t]
            for h in share:
                send_group(h)
        if t >= 2 and t - 2 >= 2 * kv_blocks:
            h = t - 2 - 2 * kv_blocks
            project(t - 2, store_q(h), True, query_scale)
            attend(h, c, True, False)
            if t == blocks:
                attend_others(0)
    for h in range(1, q_blocks):
        attend_others(h)

    def settle(d):
        pos_copy(d, c).wait_send()
        for b in range(2 * groups):
            kv_copy(b, d, c).wait_send()
        for b in range(blocks):
            x_copy(b, d).wait_send()
            s_copy(b, d).wait_send()

            def pair_sends(j, b=b):
                y_copy(b, d, j).wait_send()
                t_copy(b, d, j).wait_send()

            each(1, pairs, pair_sends)

    each(1, n, settle)


def write_out(in_ref, out_ref, sem):
    copy = pltpu.make_async_copy(in_ref, out_ref, sem)
    copy.start()
    copy.wait()


def on_device(n, grp, tokens, token_pos, norm_gain, query_weight, key_weight, value_weight):
    rows, width = tokens.shape
    depth, q_cols = query_weight.shape
    kv_cols = key_weight.shape[1]
    q_blocks, kv_blocks = q_cols // BLOCK, kv_cols // BLOCK
    blocks = q_blocks + 2 * kv_blocks
    pairs = grp // 2
    half = HEAD_DIM // 2
    freq = 10000.0 ** (-np.arange(half) * 2.0 / HEAD_DIM)
    freq = np.concatenate([freq, freq])[None, :].astype(np.float32)
    dma = pltpu.SemaphoreType.DMA
    far = max(pairs - 1, 1)
    vmem = pl.BlockSpec(memory_space=pltpu.VMEM)
    anywhere = pl.BlockSpec(memory_space=pl.ANY)
    held = [pltpu.with_memory_space_constraint(x, pltpu.HBM) for x in (tokens, query_weight, key_weight, value_weight)]
    attended = pl.pallas_call(
        functools.partial(kernel, n, grp),
        out_shape=pltpu.VMEM((rows, q_cols), jnp.bfloat16),
        in_specs=[vmem] * 3 + [pl.BlockSpec(memory_space=pltpu.HBM)] * 4,
        out_specs=vmem,
        scratch_shapes=[
            pltpu.VMEM((blocks, n * depth, BLOCK), jnp.bfloat16),
            pltpu.VMEM((rows, width), jnp.bfloat16),
            pltpu.VMEM((4 * kv_blocks, n, rows, HEAD_DIM), jnp.bfloat16),
            pltpu.VMEM((n, 8, rows), jnp.int32),
            pltpu.VMEM((q_blocks, rows, BLOCK), jnp.bfloat16),
            pltpu.VMEM((q_blocks, 2, rows, BLOCK), jnp.float32),
            pltpu.VMEM((rows, HEAD_DIM), jnp.float32),
            pltpu.VMEM((rows, HEAD_DIM), jnp.float32),
            pltpu.VMEM((rows, HEAD_DIM), jnp.float32),
            dma(()),
            dma((blocks,)),
            dma((blocks, n - 1)),
            dma((blocks, n - 1)),
            dma((blocks, n - 1, far)),
            dma((blocks, n - 1, far)),
            dma((blocks, n - 1)),
            dma((blocks, n - 1)),
            dma((blocks, n - 1, far)),
            dma((blocks, n - 1, far)),
            dma((4 * kv_blocks, n - 1)),
            dma((4 * kv_blocks, n - 1)),
            dma((n - 1,)),
            dma((n - 1,)),
        ],
        compiler_params=pltpu.CompilerParams(
            collective_id=0, has_side_effects=True, vmem_limit_bytes=44 * 1024 * 1024
        ),
    )(token_pos, freq, norm_gain, *held)
    return pl.pallas_call(
        write_out,
        out_shape=jax.ShapeDtypeStruct(attended.shape, attended.dtype),
        in_specs=[vmem],
        out_specs=anywhere,
        scratch_shapes=[dma(())],
        compiler_params=pltpu.CompilerParams(vmem_limit_bytes=4 * 1024 * 1024),
    )(attended)


def solution(mesh):
    in_specs = (
        P(("grp", "ctx"), None),
        P(("grp", "ctx")),
        P(),
        P("ctx", "tp"),
        P("ctx", "tp"),
        P("ctx", "tp"),
    )
    out_specs = P(("grp", "ctx"), "tp")
    return jax.shard_map(
        functools.partial(on_device, mesh.shape["ctx"], mesh.shape["grp"]),
        mesh=mesh, in_specs=in_specs, out_specs=out_specs, check_vma=False,
    )
```

profile of v0, /device:TPU:0, one launch (start us, length us, event | category | flops | bytes accessed | tf_op | source)
XLA Modules:
  0.0 83.4 jit_solution(7135709190672595426)
XLA Ops:
  0.0 0.0 copy-start
  0.0 0.7 copy-done
  0.7 0.0 copy-start.1
  0.7 0.7 copy-done.1
  1.4 0.0 copy-start.2
  1.4 0.7 copy-done.2
  2.1 80.3 %shard_map.73.in_ref = bf16[512,1024]{1,0:T(8,128)(2,1)S(1)} custom-call(s32[512]{0:T(512)S(1)} %copy-done.1, f32[1,128]{1,0:T(1,128)S(1)} %copy-done.2, f32[4608]{0:T(1024)S(1)} %copy-done, bf16[512,4608]{1,0:T(8,128)(2,1)} %tok_ref.1, bf16[2304,1024]{1,0:T(8,128)(2,1)} %q_ref.1, bf16[2304,512]{1,0:T(8,128)(2,1)} %k_ref.1, bf16[2304,512]{1,0:T(8,128)(2,1)} %v_ref.1), custom_call_target="tpu_custom_call" | custom-call | tf_op jit(solution)/shard_map/pallas_call | solution.py:328
  82.4 1.0 %shard_map.74 = bf16[512,1024]{1,0:T(8,128)(2,1)} custom-call(bf16[512,1024]{1,0:T(8,128)(2,1)S(1)} %shard_map.73.in_ref), custom_call_target="tpu_custom_call" | custom-call | tf_op jit(solution)/shard_map/pallas_call | solution.py:362
Async XLA Ops:
  0.0 0.7 copy-start
  0.7 0.7 copy-start.1
  1.4 0.7 copy-start.2
where the time goes:
time: 83.6 us; the launch traced here: 83.4 us
  Pallas kernels  81.3 us (97%)
  local copies, waits for them, and re-layouts  2.06 us (2%)
    pallas_call x1, Pallas kernels, on_device(): pl.pallas_call(functools.partial(kernel, n, grp), out_shape=pltpu.VMEM((r...  80.3 us
    unnamed x6, local copies, waits for them, and re-layouts  2.06 us

commit v1 on v0

--- a/solution.py
+++ b/solution.py
@@ -369,6 +369,473 @@
     )(attended)
 
 
+def pair_kernel(
+    line, pos_ref, freq_ref, gain_ref, tok_ref, q_ref, k_ref, v_ref, out_ref,
+    xbuf, oth, near, wbuf, psend, precv, acc, kbuf, vbuf, qbuf, obuf, cos_ref, sin_ref, qpos_ref,
+    factor_ref, kpos_ref, side, pos_in, freq_in, gain_in, gain_row,
+    tok_sem, w_sem, in_sem, side_send, side_recv, x_send, x_recv, up_send, up_recv, dn_send, dn_recv,
+    p_send, p_recv, r_send, r_recv, o_send, o_recv,
+):
+    c = lax.axis_index("ctx")
+    z = lax.axis_index("tp")
+    o = 1 - c
+    rows, half = oth.shape
+    heads = wbuf.shape[0]
+    mine = heads // 2
+    quarter = rows // line
+    subs = x_send.shape[0]
+    strip = quarter // subs
+    tall = math.gcd(rows, 256)
+    tiles = rows // tall
+    last = line - 1
+
+    def at_least(k):
+        return (z + line - k) // line
+
+    order = [sorted(range(line), key=lambda q, k=k: (abs(q - k), q)) for k in range(line)]
+
+    def stage_quarter(s):
+        q = order[0][s]
+        for k in range(1, line):
+            q = q + (order[k][s] - order[k - 1][s]) * at_least(k)
+        return q
+
+    def band(q, i=0, size=quarter):
+        return pl.ds(pl.multiple_of(q * quarter + i * size, strip), size)
+
+    def columns(side, i, width):
+        return pl.ds(pl.multiple_of((side * mine + i) * width, HEAD_DIM), width)
+
+    def features(side):
+        return pl.ds(pl.multiple_of(side * half, HEAD_DIM), half)
+
+    def w_copies(s):
+        side, i = (o, s) if s < mine else (c, s - mine)
+        parts = [
+            (k_ref, HEAD_DIM, 0), (v_ref, HEAD_DIM, HEAD_DIM), (q_ref, BLOCK, 2 * HEAD_DIM),
+        ]
+        return [
+            pltpu.make_async_copy(
+                ref.at[:, columns(side, i, width)], wbuf.at[s, :, pl.ds(at, width)], w_sem.at[s, p]
+            )
+            for p, (ref, width, at) in enumerate(parts)
+        ]
+
+    def tok_copies(j):
+        where = band(lax.rem(z + j, line))
+        return [
+            pltpu.make_async_copy(tok_ref.at[where, features(c)], xbuf.at[0, where], tok_sem.at[j, 0]),
+            pltpu.make_async_copy(tok_ref.at[where, features(o)], oth.at[where], tok_sem.at[j, 1]),
+        ]
+
+    def start(copies):
+        for copy in copies:
+            copy.start()
+
+    def wait(copies):
+        for copy in copies:
+            copy.wait()
+
+    def remote(src, dst, send, recv, **where):
+        return pltpu.make_async_remote_copy(
+            src_ref=src, dst_ref=dst, send_sem=send, recv_sem=recv,
+            device_id=where, device_id_type=MESH,
+        )
+
+    def x_copy(i):
+        where = band(z, i, strip)
+        return remote(oth.at[where], xbuf.at[1, where], x_send.at[i], x_recv.at[i], ctx=o)
+
+    def up_copy(e, hops):
+        where = band(z - hops - e // subs, e % subs, strip)
+        return remote(xbuf.at[1, where], xbuf.at[1, where], up_send.at[e], up_recv.at[e], tp=z + 1 - 2 * hops)
+
+    def dn_copy(e, hops):
+        where = band(z + hops + e // subs, e % subs, strip)
+        return remote(xbuf.at[1, where], xbuf.at[1, where], dn_send.at[e], dn_recv.at[e], tp=z - 1 + 2 * hops)
+
+    def side_copy():
+        return remote(side.at[0], side.at[1], side_send, side_recv, ctx=o)
+
+    def p_copy(i, t):
+        where = pl.ds(t * tall, tall)
+        return remote(psend.at[0, i, where], precv.at[1, i, where], p_send.at[i, t], p_recv.at[i, t], ctx=o)
+
+    def r_copy(i, s):
+        where = band(stage_quarter(s))
+        return remote(psend.at[1, i, where], precv.at[0, i, where], r_send.at[i, s], r_recv.at[i, s], ctx=o)
+
+    def o_copy(i, t, side):
+        where = pl.ds(t * tall, tall)
+        return remote(
+            obuf.at[i, where], out_ref.at[side * mine + i, where], o_send.at[i, t], o_recv.at[i, t], ctx=o
+        )
+
+    small = [
+        pltpu.make_async_copy(gain_ref, gain_in, in_sem.at[0]),
+        pltpu.make_async_copy(pos_ref, pos_in, in_sem.at[1]),
+        pltpu.make_async_copy(freq_ref, freq_in, in_sem.at[2]),
+    ]
+    ahead = tok_copies(0)
+    ahead[1].start()
+    start(small)
+
+    barrier = pltpu.get_barrier_semaphore()
+
+    def greet(**where):
+        pl.semaphore_signal(barrier, inc=1, device_id=where, device_id_type=MESH)
+
+    greet(ctx=o)
+
+    @pl.when(z > 0)
+    def _():
+        greet(tp=z - 1)
+
+    @pl.when(z < last)
+    def _():
+        greet(tp=z + 1)
+
+    ahead[0].start()
+    for j in range(1, line):
+        start(tok_copies(j))
+    ahead[1].wait()
+    pl.semaphore_wait(barrier, 1 + at_least(1) + 1 - at_least(last))
+    for i in range(subs):
+        x_copy(i).start()
+    for s in range(heads):
+        start(w_copies(s))
+
+    vbuf[...] = jnp.ones_like(vbuf)
+    wait(small)
+    gain_row[...] = gain_in[...][None, :]
+    side[0, 0:8, :] = jnp.broadcast_to(pos_in[...][None, :], (8, rows)).astype(jnp.float32)
+
+    def norm_rows(where):
+        own = xbuf[0, where, :].astype(jnp.float32)
+        other = oth[where, :].astype(jnp.float32)
+        total = jnp.sum(own * own, -1, keepdims=True) + jnp.sum(other * other, -1, keepdims=True)
+        factor = lax.rsqrt(total * (1.0 / (2 * half)) + 1e-06)
+        factor_ref[where, :] = jnp.broadcast_to(factor, (strip, HEAD_DIM))
+        xbuf[0, where, :] = (own * factor * gain_row[:, features(c)]).astype(jnp.bfloat16)
+
+    def norm_quarter(j):
+        wait(ahead[:1] if j == 0 else tok_copies(j))
+        each(0, subs, lambda i: norm_rows(band(lax.rem(z + j, line), i, strip)))
+
+    def norm_far(q):
+        def one(i):
+            where = band(q, i, strip)
+            raw = xbuf[1, where, :].astype(jnp.float32)
+            normed = raw * factor_ref[where, 0:1] * gain_row[:, features(c)]
+            near[pl.ds(pl.multiple_of(i * strip, strip), strip), :] = normed.astype(jnp.bfloat16)
+
+        each(0, subs, one)
+
+    def product(rows_in, s):
+        return jnp.dot(rows_in, wbuf[s], preferred_element_type=jnp.float32)
+
+    def tile(t):
+        return pl.ds(pl.multiple_of(t * tall, tall), tall)
+
+    loaded = set()
+
+    def load(s):
+        if s not in loaded:
+            loaded.add(s)
+            wait(w_copies(s))
+
+    def own_product(i):
+        load(i)
+
+        def one(t):
+            psend[0, i, tile(t), :] = product(xbuf[0, tile(t), :], i).astype(jnp.bfloat16)
+
+        each(0, tiles, one)
+        for t in range(tiles):
+            p_copy(i, t).start()
+
+    def own_local(i):
+        load(mine + i)
+
+        def one(t):
+            acc[0, i, tile(t), :] = product(xbuf[0, tile(t), :], mine + i)
+
+        each(0, tiles, one)
+
+    def far_product(i, s):
+        load(i)
+        where = band(stage_quarter(s))
+        psend[1, i, where, :] = product(near[...], i).astype(jnp.bfloat16)
+
+    def far_local(i, s):
+        load(mine + i)
+        where = band(stage_quarter(s))
+        acc[1, i, where, :] = product(near[...], mine + i)
+
+    def angles(slot):
+        where = pl.ds(slot * rows, rows)
+        lanes = side[slot, 0:1, :]
+        kpos_ref[:, where] = jnp.broadcast_to(lanes, (8, rows))
+        qpos = jnp.transpose(jnp.broadcast_to(lanes, (HEAD_DIM, rows)), (1, 0))
+        qpos_ref[where, :] = qpos
+        angle = qpos * freq_in[...]
+        lane = lax.broadcasted_iota(jnp.int32, angle.shape, 1)
+        sine = jnp.sin(angle)
+        cos_ref[where, :] = jnp.cos(angle)
+        sin_ref[where, :] = jnp.where(lane < HEAD_DIM // 2, -sine, sine)
+
+    def finish(i, slot):
+        def one(t):
+            where = tile(t)
+            at = pl.ds(pl.multiple_of(slot * rows + t * tall, tall), tall)
+            field = acc[slot, i, where, :] + precv[slot, i, where, :].astype(jnp.float32)
+            cosine, sine = cos_ref[at, :], sin_ref[at, :]
+
+            def rope(x):
+                return x * cosine + pltpu.roll(x, HEAD_DIM // 2, 1) * sine
+
+            kbuf[i, at, :] = rope(field[:, :HEAD_DIM]).astype(jnp.bfloat16)
+            vbuf[i, at, :HEAD_DIM] = field[:, HEAD_DIM : 2 * HEAD_DIM].astype(jnp.bfloat16)
+            for h in range(2):
+                one = field[:, (2 + h) * HEAD_DIM : (3 + h) * HEAD_DIM]
+                qbuf[i, at, h * HEAD_DIM : (h + 1) * HEAD_DIM] = (rope(one) * query_scale).astype(jnp.bfloat16)
+
+        each(0, tiles, one)
+
+    def attend(i, slot, t, store):
+        at = pl.ds(pl.multiple_of(slot * rows + t * tall, tall), tall)
+        for h in range(2):
+            both = None
+            for part in range(2):
+                span = pl.ds(part * rows, rows)
+                scores = lax.dot_general(
+                    qbuf[i, at, h * HEAD_DIM : (h + 1) * HEAD_DIM], kbuf[i, span, :],
+                    (((1,), (1,)), ((), ())), preferred_element_type=jnp.float32,
+                )
+                allowed = kpos_ref[0:1, span] <= qpos_ref[at, 0:1]
+                capped = jnp.tanh(scores * (1.0 / 50.0)) * (50.0 * math.log2(math.e))
+                weights = jnp.where(allowed, jnp.exp2(capped), 0.0).astype(jnp.bfloat16)
+                more = jnp.dot(weights, vbuf[i, span, :], preferred_element_type=jnp.float32)
+                both = more if both is None else both + more
+            done = (both[:, :HEAD_DIM] / both[:, HEAD_DIM:]).astype(jnp.bfloat16)
+            store(h, done)
+
+    def attend_far(i):
+        for t in range(tiles):
+            def store(h, done, t=t):
+                obuf[i, t * tall : (t + 1) * tall, h * HEAD_DIM : (h + 1) * HEAD_DIM] = done
+
+            attend(i, 1, t, store)
+            o_copy(i, t, c).start()
+
+    def attend_own(i):
+        def one(t):
+            def store(h, done):
+                out_ref[c * mine + i, tile(t), h * HEAD_DIM : (h + 1) * HEAD_DIM] = done
+
+            attend(i, 0, t, store)
+
+        each(0, tiles, one)
+
+    def pass_on(r):
+        if r < subs:
+            x_copy(r).wait_recv()
+
+            @pl.when(z < last)
+            def _():
+                up_copy(r, 0).start()
+
+            @pl.when(z > 0)
+            def _():
+                dn_copy(r, 0).start()
+
+        e = r - 1
+        if 0 <= e < last * subs:
+            @pl.when(z >= 1 + e // subs)
+            def _():
+                up_copy(e, 1).wait_recv()
+                if e + subs < last * subs:
+                    @pl.when(z < last)
+                    def _():
+                        up_copy(e + subs, 0).start()
+
+            @pl.when(z + 1 + e // subs <= last)
+            def _():
+                dn_copy(e, 1).wait_recv()
+                if e + subs < last * subs:
+                    @pl.when(z > 0)
+                    def _():
+                        dn_copy(e + subs, 0).start()
+
+    def stage(s):
+        norm_far(stage_quarter(s))
+        far_product(0, s)
+        r_copy(0, s).start()
+        for i in range(1, mine):
+            far_product(i, s)
+            early = line - 2
+            for done in range(early) if s == last - 1 else range(early, line) if s == last else ():
+                r_copy(i, done).start()
+        for i in range(mine):
+            far_local(i, s)
+
+    def far_side():
+        side_copy().wait_recv()
+        lanes = jnp.broadcast_to(side[1, 8:9, :], (HEAD_DIM, rows))
+        factor_ref[...] = jnp.transpose(lanes, (1, 0))
+
+    rounds = 1 + last * subs
+    work = {r: [] for r in range(rounds)}
+    stage_at = [subs - 1] + [s * subs for s in range(1, line)]
+    for s in range(line - 1):
+        work[stage_at[s]].append(functools.partial(stage, s))
+    work[stage_at[0]].insert(0, far_side)
+    fill = [functools.partial(own_product, i) for i in range(mine)]
+    fill += [functools.partial(angles, 0)]
+    fill += [functools.partial(own_local, i) for i in range(mine)]
+    fill += [functools.partial(angles, 1)]
+
+    for j in range(line):
+        norm_quarter(j)
+    side[0, 8:16, :] = jnp.transpose(factor_ref[...], (1, 0))[0:8, :]
+    side_copy().start()
+    for r in range(rounds):
+        pass_on(r)
+        if work[r]:
+            for task in work[r]:
+                task()
+        elif fill:
+            fill.pop(0)()
+    for task in fill:
+        task()
+
+    stage(last)
+    for i in range(mine):
+        for t in range(tiles):
+            p_copy(i, t).wait_recv()
+        finish(i, 1)
+    for i in range(mine):
+        for s in range(line):
+            r_copy(i, s).wait_recv()
+        finish(i, 0)
+        attend_far(i)
+        attend_own(i)
+    for i in range(mine):
+        for t in range(tiles):
+            o_copy(i, t, o).wait_recv()
+
+    side_copy().wait_send()
+    for i in range(subs):
+        x_copy(i).wait_send()
+    for e in range(last * subs):
+        @pl.when((z < last) & (z >= e // subs))
+        def _():
+            up_copy(e, 0).wait_send()
+
+        @pl.when((z > 0) & (z + e // subs <= last))
+        def _():
+            dn_copy(e, 0).wait_send()
+
+    for i in range(mine):
+        for t in range(tiles):
+            p_copy(i, t).wait_send()
+            o_copy(i, t, c).wait_send()
+        for s in range(line):
+            r_copy(i, s).wait_send()
+
+
+def write_heads(in_ref, out_ref, sem):
+    heads, _, width = in_ref.shape
+    copies = [
+        pltpu.make_async_copy(in_ref.at[h], out_ref.at[:, pl.ds(h * width, width)], sem.at[h])
+        for h in range(heads)
+    ]
+    for copy in copies:
+        copy.start()
+    for copy in copies:
+        copy.wait()
+
+
+def rope_freq():
+    half = HEAD_DIM // 2
+    freq = 10000.0 ** (-np.arange(half) * 2.0 / HEAD_DIM)
+    return np.concatenate([freq, freq])[None, :].astype(np.float32)
+
+
+def on_pair(line, tokens, token_pos, norm_gain, query_weight, key_weight, value_weight):
+    rows, width = tokens.shape
+    depth, q_cols = query_weight.shape
+    heads = key_weight.shape[1] // HEAD_DIM
+    mine = heads // 2
+    tiles = rows // math.gcd(rows, 256)
+    subs = max(rows // line // 32, 1)
+    dma = pltpu.SemaphoreType.DMA
+    vmem = pl.BlockSpec(memory_space=pltpu.VMEM)
+    anywhere = pl.BlockSpec(memory_space=pl.ANY)
+    hbm = pl.BlockSpec(memory_space=pltpu.HBM)
+    ins = (token_pos, jnp.asarray(rope_freq()), norm_gain, tokens, query_weight, key_weight, value_weight)
+    held = [pltpu.with_memory_space_constraint(x, pltpu.HBM) for x in ins]
+    bf16, f32 = jnp.bfloat16, jnp.float32
+    along = max((line - 1) * subs, 1)
+    attended = pl.pallas_call(
+        functools.partial(pair_kernel, line),
+        out_shape=pltpu.VMEM((heads, rows, BLOCK), bf16),
+        in_specs=[hbm] * 7,
+        out_specs=vmem,
+        scratch_shapes=[
+            pltpu.VMEM((2, rows, depth), bf16),
+            pltpu.VMEM((rows, depth), bf16),
+            pltpu.VMEM((rows // line, depth), bf16),
+            pltpu.VMEM((heads, depth, 2 * BLOCK), bf16),
+            pltpu.VMEM((2, mine, rows, 2 * BLOCK), bf16),
+            pltpu.VMEM((2, mine, rows, 2 * BLOCK), bf16),
+            pltpu.VMEM((2, mine, rows, 2 * BLOCK), f32),
+            pltpu.VMEM((mine, 2 * rows, HEAD_DIM), bf16),
+            pltpu.VMEM((mine, 2 * rows, BLOCK), bf16),
+            pltpu.VMEM((mine, 2 * rows, BLOCK), bf16),
+            pltpu.VMEM((mine, rows, BLOCK), bf16),
+            pltpu.VMEM((2 * rows, HEAD_DIM), f32),
+            pltpu.VMEM((2 * rows, HEAD_DIM), f32),
+            pltpu.VMEM((2 * rows, HEAD_DIM), f32),
+            pltpu.VMEM((rows, HEAD_DIM), f32),
+            pltpu.VMEM((8, 2 * rows), f32),
+            pltpu.VMEM((2, 16, rows), f32),
+            pltpu.VMEM((rows,), jnp.int32),
+            pltpu.VMEM((1, HEAD_DIM), f32),
+            pltpu.VMEM((width,), f32),
+            pltpu.VMEM((1, width), f32),
+            dma((line, 2)),
+            dma((heads, 3)),
+            dma((3,)),
+            dma(()),
+            dma(()),
+            dma((subs,)),
+            dma((subs,)),
+            dma((along,)),
+            dma((along,)),
+            dma((along,)),
+            dma((along,)),
+            dma((mine, tiles)),
+            dma((mine, tiles)),
+            dma((mine, line)),
+            dma((mine, line)),
+            dma((mine, tiles)),
+            dma((mine, tiles)),
+        ],
+        compiler_params=pltpu.CompilerParams(
+            collective_id=0, has_side_effects=True, vmem_limit_bytes=44 * 1024 * 1024
+        ),
+    )(*held)
+    return pl.pallas_call(
+        write_heads,
+        out_shape=jax.ShapeDtypeStruct((rows, q_cols), bf16),
+        in_specs=[vmem],
+        out_specs=anywhere,
+        scratch_shapes=[dma((heads,))],
+        compiler_params=pltpu.CompilerParams(vmem_limit_bytes=4 * 1024 * 1024),
+    )(attended)
+
+
 def solution(mesh):
     in_specs = (
         P(("grp", "ctx"), None),
@@ -379,7 +846,17 @@
         P("ctx", "tp"),
     )
     out_specs = P(("grp", "ctx"), "tp")
+    ctx, grp, line = (mesh.shape[name] for name in ("ctx", "grp", "tp"))
+
+    def local(tokens, token_pos, norm_gain, query_weight, key_weight, value_weight):
+        rows, width = tokens.shape
+        depth, kv_cols = key_weight.shape
+        heads = kv_cols // HEAD_DIM
+        paired = ctx == 2 and width == 2 * depth and heads % 2 == 0
+        paired = paired and line > 1 and rows % (line * 32) == 0
+        plan = functools.partial(on_pair, line) if paired else functools.partial(on_device, ctx, grp)
+        return plan(tokens, token_pos, norm_gain, query_weight, key_weight, value_weight)
+
     return jax.shard_map(
-        functools.partial(on_device, mesh.shape["ctx"], mesh.shape["grp"]),
-        mesh=mesh, in_specs=in_specs, out_specs=out_specs, check_vma=False,
+        local, mesh=mesh, in_specs=in_specs, out_specs=out_specs, check_vma=False,
     )

time: 83.6 us -> 76.8 us (0.919)
  Pallas kernels: 81.3 us -> 76.5 us
  local copies, waits for them, and re-layouts: 2.06 us -> 0 us
    pallas_call x2, Pallas kernels: 81.3 us -> 76.5 us  [the longest x1 75.5 us: on_pair(): pl.pallas_call(functools.partial(pair_kernel, line), out_shape=pltpu.VMEM...]
    unnamed x6 -> x0, local copies, waits for them, and re-layouts: 2.06 us -> none
where the time goes in v1:
time: 76.8 us; the launch traced here: 76.7 us
  Pallas kernels  76.5 us (100%)
    pallas_call x1, Pallas kernels, on_pair(): pl.pallas_call(functools.partial(pair_kernel, line), out_shape=pltpu.VMEM...  75.5 us

profile of v1, /device:TPU:0, one launch (start us, length us, event | category | flops | bytes accessed | tf_op | source)
XLA Modules:
  0.0 76.7 jit_solution(17942511412232002183)
XLA Ops:
  0.0 75.5 %shard_map.73.in_ref = bf16[4,512,256]{2,1,0:T(8,128)(2,1)S(1)} custom-call(s32[512]{0:T(512)} %pos_ref.1, f32[1,128]{1,0:T(1,128)} %constant.2.clone.freq_ref, f32[4608]{0:T(1024)} %gain_ref.1, bf16[512,4608]{1,0:T(8,128)(2,1)} %tok_ref.1, bf16[2304,1024]{1,0:T(8,128)(2,1)} %q_ref.1, bf16[2304,512]{1,0:T(8,128)(2,1)} %k_ref.1, bf16[2304,512]{1,0:T(8,128)(2,1)} %v_ref.1), custom_call_target="tpu_custom_call" | custom-call | tf_op jit(solution)/shard_map/pallas_call | solution.py:780
  75.5 1.0 %shard_map.74 = bf16[512,1024]{1,0:T(8,128)(2,1)} custom-call(bf16[4,512,256]{2,1,0:T(8,128)(2,1)S(1)} %shard_map.73.in_ref), custom_call_target="tpu_custom_call" | custom-call | tf_op jit(solution)/shard_map/pallas_call | solution.py:829

commit v2 on v1

--- a/solution.py
+++ b/solution.py
@@ -11,6 +11,8 @@
 
 HEAD_DIM = 128
 BLOCK = 2 * HEAD_DIM
+WAIT_QUARTERS = 3
+HELD = 2
 MESH = pl.DeviceIdType.MESH
 
 query_scale = 144.0 ** (-0.5)
@@ -379,11 +381,12 @@
     c = lax.axis_index("ctx")
     z = lax.axis_index("tp")
     o = 1 - c
+    first = lax.axis_index("grp") % 2 == 0
     rows, half = oth.shape
     heads = wbuf.shape[0]
     mine = heads // 2
     quarter = rows // line
-    subs = x_send.shape[0]
+    subs = x_recv.shape[0]
     strip = quarter // subs
     tall = math.gcd(rows, 256)
     tiles = rows // tall
@@ -416,17 +419,16 @@
         ]
         return [
             pltpu.make_async_copy(
-                ref.at[:, columns(side, i, width)], wbuf.at[s, :, pl.ds(at, width)], w_sem.at[s, p]
+                ref.at[:, columns(side, i, width)], wbuf.at[s, :, pl.ds(at, width)], w_sem.at[s]
             )
-            for p, (ref, width, at) in enumerate(parts)
+            for ref, width, at in parts
         ]
 
-    def tok_copies(j):
+    own_tokens = pltpu.make_async_copy(tok_ref.at[:, features(c)], xbuf.at[0], tok_sem.at[0])
+
+    def other_tokens(j):
         where = band(lax.rem(z + j, line))
-        return [
-            pltpu.make_async_copy(tok_ref.at[where, features(c)], xbuf.at[0, where], tok_sem.at[j, 0]),
-            pltpu.make_async_copy(tok_ref.at[where, features(o)], oth.at[where], tok_sem.at[j, 1]),
-        ]
+        return pltpu.make_async_copy(tok_ref.at[where, features(o)], oth.at[where], tok_sem.at[min(j + 1, 2)])
 
     def start(copies):
         for copy in copies:
@@ -444,31 +446,46 @@
 
     def x_copy(i):
         where = band(z, i, strip)
-        return remote(oth.at[where], xbuf.at[1, where], x_send.at[i], x_recv.at[i], ctx=o)
+        return remote(oth.at[where], xbuf.at[1, where], x_send, x_recv.at[i], ctx=o)
 
     def up_copy(e, hops):
         where = band(z - hops - e // subs, e % subs, strip)
-        return remote(xbuf.at[1, where], xbuf.at[1, where], up_send.at[e], up_recv.at[e], tp=z + 1 - 2 * hops)
+        return remote(xbuf.at[1, where], xbuf.at[1, where], up_send.at[e // subs], up_recv.at[e], tp=z + 1 - 2 * hops)
 
     def dn_copy(e, hops):
         where = band(z + hops + e // subs, e % subs, strip)
-        return remote(xbuf.at[1, where], xbuf.at[1, where], dn_send.at[e], dn_recv.at[e], tp=z - 1 + 2 * hops)
+        return remote(xbuf.at[1, where], xbuf.at[1, where], dn_send.at[e // subs], dn_recv.at[e], tp=z - 1 + 2 * hops)
+
+    pieces = rows // HEAD_DIM
+
+    def pack(first, row):
+        for k in range(pieces):
+            side[0, first + k : first + k + 1, :] = row[:, k * HEAD_DIM : (k + 1) * HEAD_DIM]
+
+    def unpack(slot, first):
+        return jnp.concatenate([side[slot, first + k : first + k + 1, :] for k in range(pieces)], -1)
+
+    def sent(ref, sem):
+        remote(ref, ref, sem, sem, ctx=o).wait_send()
+
+    def arrived(ref, sem):
+        remote(ref, ref, sem, sem, ctx=o).wait_recv()
 
     def side_copy():
         return remote(side.at[0], side.at[1], side_send, side_recv, ctx=o)
 
     def p_copy(i, t):
         where = pl.ds(t * tall, tall)
-        return remote(psend.at[0, i, where], precv.at[1, i, where], p_send.at[i, t], p_recv.at[i, t], ctx=o)
+        return remote(psend.at[0, i, where], precv.at[1, i, where], p_send.at[i], p_recv.at[i], ctx=o)
 
     def r_copy(i, s):
         where = band(stage_quarter(s))
-        return remote(psend.at[1, i, where], precv.at[0, i, where], r_send.at[i, s], r_recv.at[i, s], ctx=o)
+        return remote(psend.at[1, i, where], precv.at[0, i, where], r_send.at[i], r_recv.at[i], ctx=o)
 
     def o_copy(i, t, side):
         where = pl.ds(t * tall, tall)
         return remote(
-            obuf.at[i, where], out_ref.at[side * mine + i, where], o_send.at[i, t], o_recv.at[i, t], ctx=o
+            obuf.at[i, where], out_ref.at[where, columns(side, i, BLOCK)], o_send, o_recv, ctx=o
         )
 
     small = [
@@ -476,8 +493,7 @@
         pltpu.make_async_copy(pos_ref, pos_in, in_sem.at[1]),
         pltpu.make_async_copy(freq_ref, freq_in, in_sem.at[2]),
     ]
-    ahead = tok_copies(0)
-    ahead[1].start()
+    other_tokens(0).start()
     start(small)
 
     barrier = pltpu.get_barrier_semaphore()
@@ -495,20 +511,24 @@
     def _():
         greet(tp=z + 1)
 
-    ahead[0].start()
+    own_tokens.start()
     for j in range(1, line):
-        start(tok_copies(j))
-    ahead[1].wait()
+        other_tokens(j).start()
+    other_tokens(0).wait()
     pl.semaphore_wait(barrier, 1 + at_least(1) + 1 - at_least(last))
-    for i in range(subs):
-        x_copy(i).start()
+
+    @pl.when(first)
+    def _():
+        for i in range(subs):
+            x_copy(i).start()
+
     for s in range(heads):
         start(w_copies(s))
 
     vbuf[...] = jnp.ones_like(vbuf)
     wait(small)
     gain_row[...] = gain_in[...][None, :]
-    side[0, 0:8, :] = jnp.broadcast_to(pos_in[...][None, :], (8, rows)).astype(jnp.float32)
+    pack(0, pos_in[...][None, :].astype(jnp.float32))
 
     def norm_rows(where):
         own = xbuf[0, where, :].astype(jnp.float32)
@@ -519,7 +539,11 @@
         xbuf[0, where, :] = (own * factor * gain_row[:, features(c)]).astype(jnp.bfloat16)
 
     def norm_quarter(j):
-        wait(ahead[:1] if j == 0 else tok_copies(j))
+        if j == 0:
+            own_tokens.wait()
+        if j == 1:
+            rest = oth.at[pl.ds(0, rows - quarter)]
+            pltpu.make_async_copy(rest, rest, tok_sem.at[2]).wait()
         each(0, subs, lambda i: norm_rows(band(lax.rem(z + j, line), i, strip)))
 
     def norm_far(q):
@@ -542,7 +566,7 @@
     def load(s):
         if s not in loaded:
             loaded.add(s)
-            wait(w_copies(s))
+            pltpu.make_async_copy(wbuf.at[s], wbuf.at[s], w_sem.at[s]).wait()
 
     def own_product(i):
         load(i)
@@ -574,7 +598,7 @@
 
     def angles(slot):
         where = pl.ds(slot * rows, rows)
-        lanes = side[slot, 0:1, :]
+        lanes = unpack(slot, 0)
         kpos_ref[:, where] = jnp.broadcast_to(lanes, (8, rows))
         qpos = jnp.transpose(jnp.broadcast_to(lanes, (HEAD_DIM, rows)), (1, 0))
         qpos_ref[where, :] = qpos
@@ -631,7 +655,7 @@
     def attend_own(i):
         def one(t):
             def store(h, done):
-                out_ref[c * mine + i, tile(t), h * HEAD_DIM : (h + 1) * HEAD_DIM] = done
+                out_ref[tile(t), pl.ds(pl.multiple_of((c * mine + i) * BLOCK + h * HEAD_DIM, HEAD_DIM), HEAD_DIM)] = done
 
             attend(i, 0, t, store)
 
@@ -673,7 +697,7 @@
         r_copy(0, s).start()
         for i in range(1, mine):
             far_product(i, s)
-            early = line - 2
+            early = line - HELD
             for done in range(early) if s == last - 1 else range(early, line) if s == last else ():
                 r_copy(i, done).start()
         for i in range(mine):
@@ -681,7 +705,7 @@
 
     def far_side():
         side_copy().wait_recv()
-        lanes = jnp.broadcast_to(side[1, 8:9, :], (HEAD_DIM, rows))
+        lanes = jnp.broadcast_to(unpack(1, pieces), (HEAD_DIM, rows))
         factor_ref[...] = jnp.transpose(lanes, (1, 0))
 
     rounds = 1 + last * subs
@@ -697,7 +721,13 @@
 
     for j in range(line):
         norm_quarter(j)
-    side[0, 8:16, :] = jnp.transpose(factor_ref[...], (1, 0))[0:8, :]
+        if j == WAIT_QUARTERS - 1:
+            @pl.when(jnp.logical_not(first))
+            def _():
+                for i in range(subs):
+                    x_copy(i).start()
+
+    pack(pieces, jnp.transpose(factor_ref[...], (1, 0))[0:1, :])
     side_copy().start()
     for r in range(rounds):
         pass_on(r)
@@ -711,49 +741,30 @@
 
     stage(last)
     for i in range(mine):
-        for t in range(tiles):
-            p_copy(i, t).wait_recv()
+        arrived(precv.at[1, i], p_recv.at[i])
         finish(i, 1)
     for i in range(mine):
-        for s in range(line):
-            r_copy(i, s).wait_recv()
+        arrived(precv.at[0, i], r_recv.at[i])
         finish(i, 0)
         attend_far(i)
         attend_own(i)
+    arrived(obuf, o_recv)
+
+    side_copy().wait_send()
+    sent(xbuf.at[1, band(z)], x_send)
+    for k in range(last):
+        @pl.when((z < last) & (z >= k))
+        def _(k=k):
+            sent(xbuf.at[1, band(z - k)], up_send.at[k])
+
+        @pl.when((z > 0) & (z + k <= last))
+        def _(k=k):
+            sent(xbuf.at[1, band(z + k)], dn_send.at[k])
+
     for i in range(mine):
-        for t in range(tiles):
-            o_copy(i, t, o).wait_recv()
-
-    side_copy().wait_send()
-    for i in range(subs):
-        x_copy(i).wait_send()
-    for e in range(last * subs):
-        @pl.when((z < last) & (z >= e // subs))
-        def _():
-            up_copy(e, 0).wait_send()
-
-        @pl.when((z > 0) & (z + e // subs <= last))
-        def _():
-            dn_copy(e, 0).wait_send()
-
-    for i in range(mine):
-        for t in range(tiles):
-            p_copy(i, t).wait_send()
-            o_copy(i, t, c).wait_send()
-        for s in range(line):
-            r_copy(i, s).wait_send()
-
-
-def write_heads(in_ref, out_ref, sem):
-    heads, _, width = in_ref.shape
-    copies = [
-        pltpu.make_async_copy(in_ref.at[h], out_ref.at[:, pl.ds(h * width, width)], sem.at[h])
-        for h in range(heads)
-    ]
-    for copy in copies:
-        copy.start()
-    for copy in copies:
-        copy.wait()
+        sent(psend.at[0, i], p_send.at[i])
+        sent(psend.at[1, i], r_send.at[i])
+    sent(obuf, o_send)
 
 
 def rope_freq():
@@ -767,11 +778,9 @@
     depth, q_cols = query_weight.shape
     heads = key_weight.shape[1] // HEAD_DIM
     mine = heads // 2
-    tiles = rows // math.gcd(rows, 256)
     subs = max(rows // line // 32, 1)
     dma = pltpu.SemaphoreType.DMA
     vmem = pl.BlockSpec(memory_space=pltpu.VMEM)
-    anywhere = pl.BlockSpec(memory_space=pl.ANY)
     hbm = pl.BlockSpec(memory_space=pltpu.HBM)
     ins = (token_pos, jnp.asarray(rope_freq()), norm_gain, tokens, query_weight, key_weight, value_weight)
     held = [pltpu.with_memory_space_constraint(x, pltpu.HBM) for x in ins]
@@ -779,7 +788,7 @@
     along = max((line - 1) * subs, 1)
     attended = pl.pallas_call(
         functools.partial(pair_kernel, line),
-        out_shape=pltpu.VMEM((heads, rows, BLOCK), bf16),
+        out_shape=pltpu.VMEM((rows, q_cols), bf16),
         in_specs=[hbm] * 7,
         out_specs=vmem,
         scratch_shapes=[
@@ -799,41 +808,34 @@
             pltpu.VMEM((2 * rows, HEAD_DIM), f32),
             pltpu.VMEM((rows, HEAD_DIM), f32),
             pltpu.VMEM((8, 2 * rows), f32),
-            pltpu.VMEM((2, 16, rows), f32),
+            pltpu.VMEM((2, 2 * rows // HEAD_DIM, HEAD_DIM), f32),
             pltpu.VMEM((rows,), jnp.int32),
             pltpu.VMEM((1, HEAD_DIM), f32),
             pltpu.VMEM((width,), f32),
             pltpu.VMEM((1, width), f32),
-            dma((line, 2)),
-            dma((heads, 3)),
+            dma((3,)),
+            dma((heads,)),
             dma((3,)),
             dma(()),
             dma(()),
+            dma(()),
             dma((subs,)),
-            dma((subs,)),
+            dma((line - 1,)),
             dma((along,)),
+            dma((line - 1,)),
             dma((along,)),
-            dma((along,)),
-            dma((along,)),
-            dma((mine, tiles)),
-            dma((mine, tiles)),
-            dma((mine, line)),
-            dma((mine, line)),
-            dma((mine, tiles)),
-            dma((mine, tiles)),
+            dma((mine,)),
+            dma((mine,)),
+            dma((mine,)),
+            dma((mine,)),
+            dma(()),
+            dma(()),
         ],
         compiler_params=pltpu.CompilerParams(
             collective_id=0, has_side_effects=True, vmem_limit_bytes=44 * 1024 * 1024
         ),
     )(*held)
-    return pl.pallas_call(
-        write_heads,
-        out_shape=jax.ShapeDtypeStruct((rows, q_cols), bf16),
-        in_specs=[vmem],
-        out_specs=anywhere,
-        scratch_shapes=[dma((heads,))],
-        compiler_params=pltpu.CompilerParams(vmem_limit_bytes=4 * 1024 * 1024),
-    )(attended)
+    return attended
 
 
 def solution(mesh):
@@ -853,7 +855,7 @@
         depth, kv_cols = key_weight.shape
         heads = kv_cols // HEAD_DIM
         paired = ctx == 2 and width == 2 * depth and heads % 2 == 0
-        paired = paired and line > 1 and rows % (line * 32) == 0
+        paired = paired and line > 1 and rows % (line * 32) == 0 and rows % HEAD_DIM == 0
         plan = functools.partial(on_pair, line) if paired else functools.partial(on_device, ctx, grp)
         return plan(tokens, token_pos, norm_gain, query_weight, key_weight, value_weight)
 

time: 76.8 us -> 76 us (0.990); the launches traced: 76.7 us -> 75 us
  Pallas kernels: 76.5 us -> 74 us
  local copies, waits for them, and re-layouts: 0 us -> 0.97 us
    pallas_call x1, Pallas kernels: 75.5 us -> 74 us  [on_pair(): pl.pallas_call(functools.partial(pair_kernel, line), out_shape=pltpu.VMEM...]
    pallas_call x1 -> x0, Pallas kernels: 1 us -> none  [on_pair(): pl.pallas_call(write_heads, out_shape=jax.ShapeDtypeStruct((rows, q_cols)...]
    unnamed x0 -> x1, local copies, waits for them, and re-layouts: none -> 0.97 us
where the time goes in v2:
time: 76 us; the launch traced here: 75 us
  Pallas kernels  74 us (97%)
  local copies, waits for them, and re-layouts  0.97 us (1%)
    pallas_call x1, Pallas kernels, on_pair(): pl.pallas_call(functools.partial(pair_kernel, line), out_shape=pltpu.VMEM...  74 us

profile of v2, /device:TPU:0, one launch (start us, length us, event | category | flops | bytes accessed | tf_op | source)
XLA Modules:
  0.0 75.0 jit_solution(3598061243970843974)
XLA Ops:
  0.0 74.0 %shard_map.73 = bf16[512,1024]{1,0:T(8,128)(2,1)S(1)} custom-call(s32[512]{0:T(512)} %pos_ref.1, f32[1,128]{1,0:T(1,128)} %constant.2.clone.freq_ref, f32[4608]{0:T(1024)} %gain_ref.1, bf16[512,4608]{1,0:T(8,128)(2,1)} %tok_ref.1, bf16[2304,1024]{1,0:T(8,128)(2,1)} %q_ref.1, bf16[2304,512]{1,0:T(8,128)(2,1)} %k_ref.1, bf16[2304,512]{1,0:T(8,128)(2,1)} %v_ref.1), custom_call_target="tpu_custom_call" | custom-call | tf_op jit(solution)/shard_map/pallas_call | solution.py:789
  74.0 1.0 %copy.9 = bf16[512,1024]{1,0:T(8,128)(2,1)} copy(bf16[512,1024]{1,0:T(8,128)(2,1)S(1)} %shard_map.73) | data formatting | bytes 2097152

commit v3 on v2

--- a/solution.py
+++ b/solution.py
@@ -12,7 +12,7 @@
 HEAD_DIM = 128
 BLOCK = 2 * HEAD_DIM
 WAIT_QUARTERS = 3
-HELD = 2
+HELD = 1
 MESH = pl.DeviceIdType.MESH
 
 query_scale = 144.0 ** (-0.5)
@@ -375,8 +375,8 @@
     line, pos_ref, freq_ref, gain_ref, tok_ref, q_ref, k_ref, v_ref, out_ref,
     xbuf, oth, near, wbuf, psend, precv, acc, kbuf, vbuf, qbuf, obuf, cos_ref, sin_ref, qpos_ref,
     factor_ref, kpos_ref, side, pos_in, freq_in, gain_in, gain_row,
-    tok_sem, w_sem, in_sem, side_send, side_recv, x_send, x_recv, up_send, up_recv, dn_send, dn_recv,
-    p_send, p_recv, r_send, r_recv, o_send, o_recv,
+    tok_sem, w_sem, in_sem, side_send, side_recv, x_send, x_recv, up_send, dn_send, z_recv,
+    p_send, p_recv, r_recv, o_send, o_recv,
 ):
     c = lax.axis_index("ctx")
     z = lax.axis_index("tp")
@@ -450,11 +450,11 @@
 
     def up_copy(e, hops):
         where = band(z - hops - e // subs, e % subs, strip)
-        return remote(xbuf.at[1, where], xbuf.at[1, where], up_send.at[e // subs], up_recv.at[e], tp=z + 1 - 2 * hops)
+        return remote(xbuf.at[1, where], xbuf.at[1, where], up_send.at[e // subs], z_recv.at[e], tp=z + 1 - 2 * hops)
 
     def dn_copy(e, hops):
         where = band(z + hops + e // subs, e % subs, strip)
-        return remote(xbuf.at[1, where], xbuf.at[1, where], dn_send.at[e // subs], dn_recv.at[e], tp=z - 1 + 2 * hops)
+        return remote(xbuf.at[1, where], xbuf.at[1, where], dn_send.at[e // subs], z_recv.at[last * subs - 1 - e], tp=z - 1 + 2 * hops)
 
     pieces = rows // HEAD_DIM
 
@@ -476,11 +476,11 @@
 
     def p_copy(i, t):
         where = pl.ds(t * tall, tall)
-        return remote(psend.at[0, i, where], precv.at[1, i, where], p_send.at[i], p_recv.at[i], ctx=o)
+        return remote(psend.at[0, i, where], precv.at[1, i, where], p_send, p_recv.at[i], ctx=o)
 
     def r_copy(i, s):
         where = band(stage_quarter(s))
-        return remote(psend.at[1, i, where], precv.at[0, i, where], r_send.at[i], r_recv.at[i], ctx=o)
+        return remote(psend.at[1, i, where], precv.at[0, i, where], p_send, r_recv.at[i], ctx=o)
 
     def o_copy(i, t, side):
         where = pl.ds(t * tall, tall)
@@ -761,9 +761,7 @@
         def _(k=k):
             sent(xbuf.at[1, band(z + k)], dn_send.at[k])
 
-    for i in range(mine):
-        sent(psend.at[0, i], p_send.at[i])
-        sent(psend.at[1, i], r_send.at[i])
+    sent(psend, p_send)
     sent(obuf, o_send)
 
 
@@ -821,11 +819,9 @@
             dma(()),
             dma((subs,)),
             dma((line - 1,)),
-            dma((along,)),
             dma((line - 1,)),
             dma((along,)),
-            dma((mine,)),
-            dma((mine,)),
+            dma(()),
             dma((mine,)),
             dma((mine,)),
             dma(()),

time: 76 us -> 75.8 us (level)
  no operation moved by 1% of the time
where the time goes in v3:
time: 75.8 us; the launch traced here: 75.2 us
  Pallas kernels  74.2 us (98%)
  local copies, waits for them, and re-layouts  0.97 us (1%)
    pallas_call x1, Pallas kernels, on_pair(): pl.pallas_call(functools.partial(pair_kernel, line), out_shape=pltpu.VMEM...  74.2 us

profile of v3, /device:TPU:0, one launch (start us, length us, event | category | flops | bytes accessed | tf_op | source)
XLA Modules:
  0.0 75.2 jit_solution(524665263419598961)
XLA Ops:
  0.0 74.2 %shard_map.73 = bf16[512,1024]{1,0:T(8,128)(2,1)S(1)} custom-call(s32[512]{0:T(512)} %pos_ref.1, f32[1,128]{1,0:T(1,128)} %constant.2.clone.freq_ref, f32[4608]{0:T(1024)} %gain_ref.1, bf16[512,4608]{1,0:T(8,128)(2,1)} %tok_ref.1, bf16[2304,1024]{1,0:T(8,128)(2,1)} %q_ref.1, bf16[2304,512]{1,0:T(8,128)(2,1)} %k_ref.1, bf16[2304,512]{1,0:T(8,128)(2,1)} %v_ref.1), custom_call_target="tpu_custom_call" | custom-call | tf_op jit(solution)/shard_map/pallas_call | solution.py:787
  74.2 1.0 %copy.9 = bf16[512,1024]{1,0:T(8,128)(2,1)} copy(bf16[512,1024]{1,0:T(8,128)(2,1)S(1)} %shard_map.73) | data formatting | bytes 2097152
